TPU v7x, 32 devices: a whole 2x2x4 slice. The times are simulated.
32 devices in a mesh: dp: 4 (over y, x), vocab: 8 (over z, core).
Axes of the slice: x: 2, y: 2, z: 4, core: 2. Of those that a mesh axis runs over, the one named last changes fastest.
Arguments:
- hidden: bfloat16 [512, 8192], P('dp', 'vocab'), may hold values from -20 to 20
- weight: bfloat16 [8192, 4752], P('dp', 'vocab'), may hold values from -0.198873782 to 0.198873782
- targets: int32 [512], P('dp'), may hold values from 0 to 4751
- loss_mask: int32 [512], P('dp'), may hold values 0 or 1
Outputs:
- grad_hidden: bfloat16 [512, 8192], P('dp', 'vocab')
- grad_weight: bfloat16 [8192, 4752], P('dp', 'vocab')
- token_loss: float32 [512], P('dp')
- grad_norm: float32 [], replicated
All inputs are finite; a program needn't handle non-finite values. No bound on the sum of `loss_mask` on one device may be relied on, other than what follows from the above.
Results may differ from a plain program's by a relative error of at most 0.0034.
Values may be sent and summed in bfloat16 or wider, within the bound.
A program may use at most 128 MiB of HBM per device.

v0:
```python
import jax
import jax.numpy as jnp
from jax import lax
from jax.sharding import PartitionSpec as P

loss_scale = 16.0


def on_device(hidden, weight, targets, loss_mask):
    shard_width = weight.shape[1]
    col_offset = lax.axis_index("vocab") * shard_width
    full_hidden = lax.all_gather(hidden, "vocab", axis=1, tiled=True)
    hidden_block = lax.all_to_all(full_hidden, "dp", split_axis=1, concat_axis=0, tiled=True)
    full_weight = lax.all_gather(weight, "dp", axis=0, tiled=True)
    logits = jnp.dot(full_hidden, full_weight, preferred_element_type=jnp.float32)
    row_targets, row_mask = (targets, loss_mask)
    local_col = row_targets - col_offset
    onehot = (lax.broadcasted_iota(jnp.int32, logits.shape, 1) == local_col[:, None]).astype(
        jnp.float32
    )
    target_local = jnp.sum(logits * onehot, axis=1)
    local_top = jnp.max(logits, axis=1)
    row_top = lax.pmax(local_top, "vocab")
    local_sum = jnp.sum(jnp.exp(logits - row_top[:, None]), axis=1)
    exp_sum, target_logit = lax.psum((local_sum, target_local), "vocab")
    log_total = row_top + jnp.log(exp_sum)
    row_keep = row_mask.astype(jnp.float32)
    loss_rows = row_keep * (log_total - target_logit)
    softmax = jnp.exp(logits - log_total[:, None])
    dlogits = (loss_scale * row_keep[:, None] * (softmax - onehot)).astype(jnp.bfloat16)
    dlog_all = lax.all_gather(dlogits, "dp", axis=0, tiled=True)
    hidden_terms = lax.dot_general(
        dlogits, full_weight, (((1,), (1,)), ((), ())), preferred_element_type=jnp.float32
    )
    hidden_grad_full = lax.psum_scatter(hidden_terms, "vocab", scatter_dimension=1, tiled=True)
    weight_grad_full = lax.dot_general(
        hidden_block, dlog_all, (((0,), (0,)), ((), ())), preferred_element_type=jnp.float32
    )
    local_squares = jnp.sum(weight_grad_full * weight_grad_full) + jnp.sum(
        hidden_grad_full * hidden_grad_full
    )
    squares_total = lax.psum(local_squares, ("dp", "vocab"))
    return (
        hidden_grad_full.astype(jnp.bfloat16),
        weight_grad_full.astype(jnp.bfloat16),
        loss_rows,
        jnp.sqrt(squares_total),
    )


def solution(mesh):
    placed = (P("dp", "vocab"), P("dp", "vocab"), P("dp"), P("dp"))
    return jax.shard_map(
        on_device,
        mesh=mesh,
        in_specs=placed,
        out_specs=(P("dp", "vocab"), P("dp", "vocab"), P("dp"), P()),
        check_vma=False,
    )
```

profile of v0, /device:TPU:0, one launch (start us, length us, event | category | flops | bytes accessed | tf_op | source)
XLA Modules:
  0.0 284.9 jit_solution(2477782353101069427)
XLA Ops:
  7.2 0.0 copy-start.2
  7.2 0.0 all-gather.3.cloned.1.call-start
  7.2 1.8 copy.8
  9.0 0.0 all-gather.3.cloned.1.call-update
  9.0 0.0 all-gather.5.cloned.1.call-start
  9.1 0.7 all-gather.5.cloned.1.call-update
  9.8 0.0 reduce-scatter.2.cloned.1.call-start
  9.8 0.0 copy-done.2
  9.9 0.0 copy-start.1
  9.9 32.2 %all-gather.3.cloned.1.call-done = bf16[128,8192]{0,1:T(8,128)(2,1)} async-done(((bf16[128,1024]{0,1:T(8,128)(2,1)}), bf16[128,8192]{0,1:T(8,128)(2,1)}) %all-gather.3.cloned.1.call-update) | async-done | bytes 2097168 | tf_op jit(solution)/shard_map/all_gather | solution.py:12
  42.1 100.7 %all-gather.5.cloned.1.call-done = bf16[8192,594]{0,1:T(8,128)(2,1)} async-done(((bf16[2048,594]{0,1:T(8,128)(2,1)}), bf16[8192,594]{0,1:T(8,128)(2,1)}) %all-gather.5.cloned.1.call-update) | async-done | bytes 9732112 | tf_op jit(solution)/shard_map/all_gather | solution.py:14
  142.8 6.2 %fusion = (f32[128]{0:T(128)S(1)}, f32[128,594]{0,1:T(8,128)S(1)}) fusion(bf16[128,8192]{0,1:T(8,128)(2,1)} %all-gather.3.cloned.1.call-done, bf16[8192,594]{0,1:T(8,128)(2,1)} %all-gather.5.cloned.1.call-done), kind=kOutput, calls=%fused_computation.11 | convolution fusion | flops 1245784192 | bytes 12133888 | tf_op jit(solution)/shard_map/dot_general | solution.py:15
  149.0 16.2 %pmax.7 = f32[128]{0:T(128)S(1)} all-reduce(f32[128]{0:T(128)S(1)} %get-tuple-element.15), channel_id=1, replica_groups=mesh['dp'=4,'vocab'=8] {'vocab'}, use_global_device_ids=true, to_apply=%region_1.0 | all-reduce | flops 128 | bytes 1024 | tf_op jit(solution)/shard_map/pmax | solution.py:23
  165.2 0.1 select_reduce_fusion
  165.3 13.6 %all-reduce = (f32[128]{0:T(128)S(1)}, f32[128]{0:T(128)S(1)}) all-reduce(f32[128]{0:T(128)S(1)} %get-tuple-element.5, f32[128]{0:T(128)S(1)} %get-tuple-element.4), channel_id=1, replica_groups=mesh['dp'=4,'vocab'=8] {'vocab'}, use_global_device_ids=true, to_apply=%region_3.0 | all-reduce | flops 256 | bytes 2048 | tf_op jit(solution)/shard_map/psum | solution.py:25
  178.9 0.0 copy-done.1
  178.9 0.5 subtract_multiply_fusion
  179.4 0.1 multiply_convert_fusion
  179.5 8.0 %fusion.1 = f32[128,8192]{1,0:T(8,128)} fusion(bf16[128,594]{0,1:T(8,128)(2,1)S(1)} %multiply_convert_fusion, bf16[8192,594]{0,1:T(8,128)(2,1)} %all-gather.5.cloned.1.call-done), kind=kOutput, calls=%fused_computation.12 | convolution fusion | flops 1245708288 | bytes 14078464 | tf_op jit(solution)/shard_map/dot_general | solution.py:32
  187.5 0.0 copy-start
  187.5 0.0 reduce-scatter.2.cloned.1.call-update
  187.6 1.6 copy-done
  189.1 28.9 %all_to_all.19 = bf16[128,4,2048]{0,2,1:T(8,128)(2,1)} all-to-all(bf16[128,4,2048]{0,2,1:T(8,128)(2,1)S(1)} %bitcast.11), channel_id=1, replica_groups=mesh['dp'=4,'vocab'=8] {'dp'}, dimensions={1} | all-to-all | bytes 4194304 | tf_op jit(solution)/shard_map/all_to_all | solution.py:13
  218.1 2.9 %copy.9 = bf16[4,128,2048]{2,1,0:T(8,128)(2,1)S(1)} copy(bf16[4,128,2048]{1,2,0:T(8,128)(2,1)} %bitcast.12) | data formatting | bytes 4194304 | tf_op jit(solution)/shard_map/all_to_all | solution.py:13
  221.0 9.9 %all_gather.11 = bf16[512,594]{0,1:T(8,128)(2,1)S(1)} all-gather(bf16[128,594]{0,1:T(8,128)(2,1)S(1)} %multiply_convert_fusion), channel_id=1, replica_groups=mesh['dp'=4,'vocab'=8] {'dp'}, dimensions={0}, use_global_device_ids=true | all-gather | bytes 760320 | tf_op jit(solution)/shard_map/all_gather | solution.py:31
  230.9 3.6 %multiply_reduce_fusion = (f32[]{:T(128)}, bf16[2048,594]{0,1:T(8,128)(2,1)}) fusion(bf16[512,594]{0,1:T(8,128)(2,1)S(1)} %all_gather.11, bf16[512,2048]{1,0:T(8,128)(2,1)S(1)} %bitcast.13), kind=kOutput, calls=%fused_computation | convolution fusion | flops 1249357824 | bytes 5138436 | tf_op jit(solution)/shard_map/dot_general | solution.py:36
  234.5 0.3 reduce-scatter.2.cloned.1.call-done
  234.9 2.6 multiply_reduce_fusion.1
  238.8 37.8 %psum.23 = f32[]{:T(128)} all-reduce(f32[]{:T(128)S(6)} %add.15), channel_id=1, replica_groups=mesh['dp'=4,'vocab'=8] {'dp','vocab'}, use_global_device_ids=true, to_apply=%region_9.0 | all-reduce | flops 1 | bytes 8 | tf_op jit(solution)/shard_map/psum | solution.py:42
  (1 shorter events, 0.0 us)
Async XLA Ops:
  7.2 2.7 copy-start.2
  7.2 34.9 %all-gather.3.cloned.1.call-start = ((), (), s32[]{:S(2)}) async-start(), calls=%async_computation.2 | async-start | bytes 2359296 | tf_op jit(solution)/shard_map/all_gather | solution.py:12
  9.0 133.8 %all-gather.5.cloned.1.call-start = ((), (), s32[]{:S(2)}) async-start(), calls=%async_computation.3 | async-start | bytes 12288000 | tf_op jit(solution)/shard_map/all_gather | solution.py:14
  9.8 225.1 %reduce-scatter.2.cloned.1.call-start = ((), (), s32[]{:S(2)}) async-start(), calls=%async_computation.4 | async-start | bytes 4718592 | tf_op jit(solution)/shard_map/reduce_scatter | solution.py:35
  9.9 169.0 %copy-start.1 = (s32[128]{0:T(128)S(1)}, s32[128]{0:T(128)}, u32[]{:S(2)}) copy-start(s32[128]{0:T(128)} %param.7) | copy-start | bytes 1540
  187.5 1.6 copy-start
Sparse Core Ops, SparseCore 0:
  10.2 31.8 all-gather.2
  43.9 98.8 all-gather.4
  187.7 47.1 reduce-scatter.1
where the time goes:
time: 286 us; the launch traced here: 285 us
  waiting for transfers between devices  134 us (47%)
  blocking collectives  106 us (37%)
  matrix products  17.8 us (6%)
  between operations  17 us (6%)
  local copies, waits for them, and re-layouts  6.3 us (2%)
  other arithmetic  3.29 us (1%)
    all_gather x1, waiting for transfers between devices, on_device(): full_weight = lax.all_gather(weight, 'dp', axis=0, tiled=True)  101 us
    psum x1, blocking collectives, on_device(): squares_total = lax.psum(local_squares, ('dp', 'vocab'))  37.8 us
    all_gather x1, waiting for transfers between devices, on_device(): full_hidden = lax.all_gather(hidden, 'vocab', axis=1, tiled=True)  32.2 us
    all_to_all x1, blocking collectives, on_device(): lax.all_to_all(full_hidden, 'dp', split_axis=1, concat_axis=0, tiled=True)  28.9 us
    pmax x1, blocking collectives, on_device(): row_top = lax.pmax(local_top, 'vocab')  16.2 us
    psum x1, blocking collectives, on_device(): exp_sum, target_logit = lax.psum((local_sum, target_local), 'vocab')  13.6 us
    all_gather x1, blocking collectives, on_device(): dlog_all = lax.all_gather(dlogits, 'dp', axis=0, tiled=True)  9.93 us
    dot_general x1, matrix products, on_device(): lax.dot_general(dlogits, full_weight, (((1,), (1,)), ((), ())), preferred...  8.01 us
  transfers between devices with their start and end apart: 3, of which 3 were waited for; matrix products, arithmetic and copies ran while one was open for 2% of the time, Pallas kernels for 0%

commit v1 on v0

v1 whole, which is shorter than its diff:
```python
import functools

import jax
import jax.numpy as jnp
from jax import lax
from jax.experimental import pallas as pl
from jax.experimental.pallas import tpu as pltpu
from jax.sharding import PartitionSpec as P

loss_scale = 16.0
MESH = pl.DeviceIdType.MESH
f32 = jnp.float32
bf16 = jnp.bfloat16


def dot_nn(a, b):
    return jnp.dot(a, b, preferred_element_type=f32)


def dot_nt(a, b):
    return lax.dot_general(a, b, (((1,), (1,)), ((), ())), preferred_element_type=f32)


def dot_tn(a, b):
    return lax.dot_general(a, b, (((0,), (0,)), ((), ())), preferred_element_type=f32)


def kernel(
    n, nv, cpc,
    hid, w, tgt, keep,
    hg_out, wg_out, loss_out, norm_out,
    gat, hb, lp, lr, st, sr, dall, ps, pr, gs, g1, g2, n1s, n1, n2s, n2,
    h1_s, h1_r, h2_s, hb_r, h3_s, l_s, l_r, s_s, s_r, d_s, d_r,
    p_s, p_r, g1_s, g1_r, g2_s, g2_r, n1_s, n1_r, n2_s, n2_r,
):
    T, F = hid.shape
    V = w.shape[1]
    bpd = nv // n
    zpd = bpd // cpc
    nz = nv // cpc
    k = lax.axis_index("dp")
    j = lax.axis_index("vocab")
    z, c = j // cpc, j % cpc
    sends = []

    def push(src, dst, ss, rs, dp, vocab):
        copy = pltpu.make_async_remote_copy(
            src_ref=src, dst_ref=dst, send_sem=ss, recv_sem=rs,
            device_id={"dp": dp, "vocab": vocab}, device_id_type=MESH,
        )
        copy.start()
        sends.append((src, ss))

    def local(src, dst, sem):
        pltpu.make_async_copy(src, dst, sem).start()

    def arrived(dst, sem):
        pltpu.make_async_copy(dst, dst, sem).wait()

    def turn(s, base, size):
        return lax.rem(base + s, size)

    row_order = list(range(1, n)) + [0]

    barrier = pltpu.get_barrier_semaphore()
    for s in range(1, nv):
        pl.semaphore_signal(barrier, inc=1, device_id={"dp": k, "vocab": turn(s, j, nv)}, device_id_type=MESH)
    for s in range(1, n):
        pl.semaphore_signal(barrier, inc=1, device_id={"dp": turn(s, k, n), "vocab": j}, device_id_type=MESH)
    pl.semaphore_wait(barrier, nv + n - 2)

    for s in range(1, nz):
        to = turn(s, z, nz)
        push(hid, gat.at[z], h1_s.at[s], h1_r.at[z], k, to * cpc + c)
    local(hid, gat.at[z], h1_r.at[z])

    for s in row_order:
        i = turn(s, k, n)
        for q in range(zpd):
            src = gat.at[i * zpd + q]
            arrived(src, h1_r.at[i * zpd + q])
            bl = q * cpc + c
            if s:
                push(src, hb.at[bl, k], h2_s.at[s, q], hb_r.at[k, bl], i, j)
            else:
                local(src, hb.at[bl, k], hb_r.at[k, bl])

    for s in [0] + list(range(1, n)):
        t = turn(s, k, n)
        for q in range(zpd):
            bl = q * cpc + c
            arrived(hb.at[bl, t], hb_r.at[t, bl])
            for d in range(1, cpc):
                push(hb.at[bl, t], hb.at[bl, t], h3_s.at[s, q, d], hb_r.at[t, bl], k, z * cpc + turn(d, c, cpc))

    for s in row_order:
        t = turn(s, k, n)
        for q in range(zpd):
            for d in range(1, cpc):
                bl = q * cpc + turn(d, c, cpc)
                arrived(hb.at[bl, t], hb_r.at[t, bl])
        total = dot_nn(hb[0, t], w[0:F, :])
        for bl in range(1, bpd):
            total += dot_nn(hb[bl, t], w[bl * F:(bl + 1) * F, :])
        if s:
            lp[s - 1] = total
            push(lp.at[s - 1], lr.at[s - 1], l_s.at[s - 1], l_r.at[s - 1], t, j)
    logits = total
    for s in range(n - 1):
        arrived(lr.at[s], l_r.at[s])
        logits += lr[s]

    def to_column(row):
        return jnp.transpose(jnp.broadcast_to(row, (128, T)))[:, :1]

    target_col = to_column(tgt[...].astype(f32)).astype(jnp.int32) - j * V
    onehot = lax.broadcasted_iota(jnp.int32, (T, V), 1) == target_col
    top = jnp.max(logits, axis=1, keepdims=True)
    part = jnp.sum(jnp.exp(logits - top), axis=1, keepdims=True)
    hit = jnp.sum(jnp.where(onehot, logits, 0.0), axis=1, keepdims=True)
    lane = lax.broadcasted_iota(jnp.int32, (T, 128), 1)
    packed = jnp.where(lane == 0, top, jnp.where(lane == 1, part, hit))
    mine = jnp.transpose(packed)[:8, :]
    st[...] = mine
    sr[j] = mine
    for s in range(1, nv):
        push(st, sr.at[j], s_s.at[s], s_r.at[j], k, turn(s, j, nv))
    for s in range(1, nv):
        frm = turn(s, j, nv)
        arrived(sr.at[frm], s_r.at[frm])
    stats = sr[...]
    tops, parts, hits = stats[:, 0, :], stats[:, 1, :], stats[:, 2, :]
    row_top = jnp.max(tops, axis=0, keepdims=True)
    exp_sum = jnp.sum(parts * jnp.exp(tops - row_top), axis=0, keepdims=True)
    target_logit = jnp.sum(hits, axis=0, keepdims=True)
    log_total = row_top + jnp.log(exp_sum)
    row_keep = keep[...].astype(f32)
    loss_out[...] = row_keep * (log_total - target_logit)

    soft = jnp.exp(logits - to_column(log_total))
    dl = (loss_scale * to_column(row_keep) * (soft - jnp.where(onehot, 1.0, 0.0))).astype(bf16)
    dall[k] = dl
    for s in range(1, n):
        push(dall.at[k], dall.at[k], d_s.at[s], d_r.at[k], turn(s, k, n), j)

    for s in [0] + list(range(1, n)):
        t = turn(s, k, n)
        if s:
            arrived(dall.at[t], d_r.at[t])
        for d in range(1, cpc):
            other = turn(d, c, cpc)
            for q in range(zpd):
                off = pl.multiple_of((q * cpc + other) * F, F)
                ps[s, d - 1, q] = dot_nt(dall[t], w[pl.ds(off, F), :])
            push(ps.at[s, d - 1], pr.at[s, d - 1], p_s.at[s, d - 1], p_r.at[s, d - 1], k, z * cpc + other)
    for s in row_order:
        t = turn(s, k, n)
        for d in range(1, cpc):
            arrived(pr.at[s, d - 1], p_r.at[s, d - 1])
        for q in range(zpd):
            off = pl.multiple_of((q * cpc + c) * F, F)
            part_sum = dot_nt(dall[t], w[pl.ds(off, F), :])
            for d in range(1, cpc):
                part_sum += pr[s, d - 1, q]
            gs[s, q] = part_sum.astype(bf16)
        if s:
            push(gs.at[s], g1.at[k], g1_s.at[s], g1_r.at[k], t, j)
        else:
            local(gs.at[s], g1.at[k], g1_r.at[k])

    grads = dall[...].reshape(n * T, V)
    squares = jnp.zeros((1, V), f32)
    rows = bpd * F
    tile = min(F, 256)
    per = rows // tile // n
    done = 0
    for s in row_order[-1:] + row_order[:-1]:
        def step(m, acc):
            first = m * tile
            bl = first // F
            col = pl.multiple_of(lax.rem(first, F), tile)
            lhs = hb[bl, :, :, pl.ds(col, tile)] if F > tile else hb[bl]
            g = dot_tn(lhs.reshape(n * T, tile), grads)
            wg_out[pl.ds(pl.multiple_of(first, tile), tile), :] = g.astype(bf16)
            return acc + jnp.sum(g * g, axis=0, keepdims=True)

        squares = lax.fori_loop(done, done + per, step, squares)
        done += per
        i = turn(s, k, n)
        arrived(g1.at[i], g1_r.at[i])
        for q in range(zpd):
            to = i * zpd + q

            @pl.when(to != z)
            def _():
                pltpu.make_async_remote_copy(
                    src_ref=g1.at[i, q], dst_ref=g2.at[z], send_sem=g2_s.at[s, q], recv_sem=g2_r.at[z],
                    device_id={"dp": k, "vocab": to * cpc + c}, device_id_type=MESH,
                ).start()

            @pl.when(to == z)
            def _():
                pltpu.make_async_copy(g1.at[i, q], g2.at[z], g2_r.at[z]).start()

    total = None
    for src in range(nz):
        arrived(g2.at[src], g2_r.at[src])
        term = g2[src].astype(f32)
        total = term if total is None else total + term
    hg_out[...] = total.astype(bf16)

    both = jnp.sum(squares) + jnp.sum(total * total)
    value = jnp.full((8, 128), both, f32)
    n1s[...] = value
    n1[j] = value
    for s in range(1, nv):
        push(n1s, n1.at[j], n1_s.at[s], n1_r.at[j], k, turn(s, j, nv))
    for s in range(1, nv):
        frm = turn(s, j, nv)
        arrived(n1.at[frm], n1_r.at[frm])
    value = n1[0]
    for a in range(1, nv):
        value = value + n1[a]
    n2s[...] = value
    n2[k] = value
    for s in range(1, n):
        push(n2s, n2.at[k], n2_s.at[s], n2_r.at[k], turn(s, k, n), j)
    for s in range(1, n):
        frm = turn(s, k, n)
        arrived(n2.at[frm], n2_r.at[frm])
    value = n2[0]
    for a in range(1, n):
        value = value + n2[a]
    norm_out[...] = jnp.sqrt(value)

    for src, ss in sends:
        pltpu.make_async_copy(src, src, ss).wait()
    for s in range(n):
        i = turn(s, k, n)
        for q in range(zpd):
            @pl.when(i * zpd + q != z)
            def _():
                pltpu.make_async_copy(g1.at[i, q], g1.at[i, q], g2_s.at[s, q]).wait()


def on_device(n, nv, hidden, weight, targets, loss_mask):
    T, F = hidden.shape
    R, V = weight.shape
    bpd = nv // n
    cpc = 2 if bpd % 2 == 0 else 1
    zpd, nz = bpd // cpc, nv // cpc
    dma = pltpu.SemaphoreType.DMA
    vmem = pl.BlockSpec(memory_space=pltpu.VMEM)
    others = max(cpc - 1, 1)
    hg, wg, loss, norm = pl.pallas_call(
        functools.partial(kernel, n, nv, cpc),
        out_shape=(
            jax.ShapeDtypeStruct((T, F), bf16),
            jax.ShapeDtypeStruct((R, V), bf16),
            jax.ShapeDtypeStruct((1, T), f32),
            jax.ShapeDtypeStruct((8, 128), f32),
        ),
        in_specs=[vmem] * 4,
        out_specs=(vmem,) * 4,
        scratch_shapes=[
            pltpu.VMEM((nz, T, F), bf16),
            pltpu.VMEM((bpd, n, T, F), bf16),
            pltpu.VMEM((n - 1, T, V), f32),
            pltpu.VMEM((n - 1, T, V), f32),
            pltpu.VMEM((8, T), f32),
            pltpu.VMEM((nv, 8, T), f32),
            pltpu.VMEM((n, T, V), bf16),
            pltpu.VMEM((n, others, zpd, T, F), f32),
            pltpu.VMEM((n, others, zpd, T, F), f32),
            pltpu.VMEM((n, zpd, T, F), bf16),
            pltpu.VMEM((n, zpd, T, F), bf16),
            pltpu.VMEM((nz, T, F), bf16),
            pltpu.VMEM((8, 128), f32),
            pltpu.VMEM((nv, 8, 128), f32),
            pltpu.VMEM((8, 128), f32),
            pltpu.VMEM((n, 8, 128), f32),
            dma((nz,)), dma((nz,)),
            dma((n, zpd)), dma((n, bpd)), dma((n, zpd, cpc)),
            dma((n,)), dma((n,)),
            dma((nv,)), dma((nv,)),
            dma((n,)), dma((n,)),
            dma((n, others)), dma((n, others)),
            dma((n,)), dma((n,)),
            dma((n, zpd)), dma((nz,)),
            dma((nv,)), dma((nv,)),
            dma((n,)), dma((n,)),
        ],
        compiler_params=pltpu.CompilerParams(
            collective_id=0, has_side_effects=True, vmem_limit_bytes=60 * 1024 * 1024
        ),
    )(hidden, weight, targets.reshape(1, T), loss_mask.reshape(1, T))
    return hg, wg, loss.reshape(T), norm[0, 0]


def solution(mesh):
    placed = (P("dp", "vocab"), P("dp", "vocab"), P("dp"), P("dp"))
    return jax.shard_map(
        functools.partial(on_device, mesh.shape["dp"], mesh.shape["vocab"]),
        mesh=mesh,
        in_specs=placed,
        out_specs=(P("dp", "vocab"), P("dp", "vocab"), P("dp"), P()),
        check_vma=False,
    )
```

time: 286 us -> 139 us (0.49)
  waiting for transfers between devices: 134 us -> 0 us
  Pallas kernels: 0 us -> 127 us
  blocking collectives: 106 us -> 0 us
  matrix products: 17.8 us -> 0 us
  between operations: 17 us -> 0.65 us
  local copies, waits for them, and re-layouts: 6.3 us -> 11.1 us
  other arithmetic: 3.29 us -> 0 us
    all_gather x2 -> x0, waiting for transfers between devices: 133 us -> none  [the longest x1 101 us: on_device(): full_weight = lax.all_gather(weight, 'dp', axis=0, tiled=True)]
    pallas_call x0 -> x1, Pallas kernels: none -> 127 us  [on_device(): pl.pallas_call(functools.partial(kernel, n, nv, cpc), out_shape=(jax.Shap...]
    psum x2 -> x0, blocking collectives: 51.4 us -> none  [the longest x1 37.8 us: on_device(): squares_total = lax.psum(local_squares, ('dp', 'vocab'))]
    all_to_all x1 -> x0, blocking collectives: 28.9 us -> none  [on_device(): lax.all_to_all(full_hidden, 'dp', split_axis=1, concat_axis=0, tiled=True)]
    dot_general x3 -> x0, matrix products: 17.8 us -> none  [the longest x1 8.01 us: on_device(): lax.dot_general(dlogits, full_weight, (((1,), (1,)), ((), ())), preferred...]
    pmax x1 -> x0, blocking collectives: 16.2 us -> none  [on_device(): row_top = lax.pmax(local_top, 'vocab')]
    all_gather x1 -> x0, blocking collectives: 9.93 us -> none  [on_device(): dlog_all = lax.all_gather(dlogits, 'dp', axis=0, tiled=True)]
    unnamed x7 -> x8, local copies, waits for them, and re-layouts: 3.37 us -> 9.9 us
  transfers between devices with their start and end apart: 3 -> 0, of which waited for: 3 -> 0; matrix products, arithmetic and copies ran while one was open for 2% -> 0% of each run, Pallas kernels for 0% -> 0%
where the time goes in v1:
time: 139 us
  Pallas kernels  127 us (91%)
  local copies, waits for them, and re-layouts  11.1 us (8%)
    pallas_call x1, Pallas kernels, on_device(): pl.pallas_call(functools.partial(kernel, n, nv, cpc), out_shape=(jax.Shap...  127 us
    unnamed x8, local copies, waits for them, and re-layouts  9.9 us

profile of v1, /device:TPU:0, one launch (start us, length us, event | category | flops | bytes accessed | tf_op | source)
XLA Modules:
  0.0 138.6 jit_solution(2676223113102166196)
XLA Ops:
  0.6 4.3 %copy.8.w = bf16[2048,594]{1,0:T(8,128)(2,1)} copy(bf16[2048,594]{0,1:T(8,128)(2,1)} %param.5) | data formatting | bytes 4866048 | tf_op args[1]
  5.0 126.8 %shard_map.75 = (bf16[128,1024]{1,0:T(8,128)(2,1)}, bf16[2048,594]{1,0:T(8,128)(2,1)}, f32[1,128]{1,0:T(1,128)}, f32[8,128]{1,0:T(8,128)}) custom-call(bf16[128,1024]{1,0:T(8,128)(2,1)} %hid.1, bf16[2048,594]{1,0:T(8,128)(2,1)} %copy.8.w, s32[1,128]{1,0:T(1,128)} %bitcast.4, s32[1,128]{1,0:T(1,128)} %bitcast.5), custom_call_target="tpu_custom_call" | custom-call | tf_op jit(solution)/shard_map/pallas_call | solution.py:255
  131.8 0.0 copy-start
  131.8 1.2 slice.3
  133.0 0.0 copy-start.1
  133.0 4.3 %copy.9 = bf16[2048,594]{0,1:T(8,128)(2,1)} copy(bf16[2048,594]{1,0:T(8,128)(2,1)} %get-tuple-element.13) | data formatting | bytes 4866048
  137.4 0.0 copy-done
  137.4 0.7 copy.12
  138.1 0.0 copy-done.1
  138.1 0.5 copy.13
Async XLA Ops:
  131.8 5.6 %copy-start = (bf16[128,1024]{1,0:T(8,128)(2,1)S(1)}, bf16[128,1024]{1,0:T(8,128)(2,1)}, u32[]{:S(2)}) copy-start(bf16[128,1024]{1,0:T(8,128)(2,1)} %get-tuple-element.20) | copy-start | bytes 786436
  133.0 5.0 %copy-start.1 = (f32[1,128]{1,0:T(1,128)S(1)}, f32[1,128]{1,0:T(1,128)}, u32[]{:S(2)}) copy-start(f32[1,128]{1,0:T(1,128)} %get-tuple-element.10) | copy-start | bytes 1540

commit v2 on v1

v2 whole, which is shorter than its diff:
```python
import functools

import jax
import jax.numpy as jnp
from jax import lax
from jax.experimental import pallas as pl
from jax.experimental.pallas import tpu as pltpu
from jax.sharding import PartitionSpec as P

loss_scale = 16.0
MESH = pl.DeviceIdType.MESH
f32 = jnp.float32
bf16 = jnp.bfloat16


def dot_nn(a, b):
    return jnp.dot(a, b, preferred_element_type=f32)


def dot_nt(a, b):
    return lax.dot_general(a, b, (((1,), (1,)), ((), ())), preferred_element_type=f32)


def dot_tn(a, b):
    return lax.dot_general(a, b, (((0,), (0,)), ((), ())), preferred_element_type=f32)


def kernel(
    n, nv, cpc, nc, ng,
    hid, w_in, tgt, keep,
    hg_out, wg_out, loss_out, norm_out,
    w, wg, gat, hb, lp, lr, st, sr, dall, ps, pr, gs, g1, g2, n1s, n1, n2s, n2,
    h1_s, h1_r, h2_s, hb_r, h3_s, l_s, l_r, s_s, s_r, d_s, d_r,
    io, p_s, p_r, g1_s, g1_r, g2_s, g2_r, n1_s, n1_r, n2_s, n2_r,
):
    T, F = hid.shape
    V = w.shape[0]
    Tc, Tg = T // nc, T // ng
    bpd = nv // n
    zpd = bpd // cpc
    nz = nv // cpc
    k = lax.axis_index("dp")
    j = lax.axis_index("vocab")
    z, c = j // cpc, j % cpc
    sends = []

    def push(src, dst, ss, rs, dp, vocab):
        copy = pltpu.make_async_remote_copy(
            src_ref=src, dst_ref=dst, send_sem=ss, recv_sem=rs,
            device_id={"dp": dp, "vocab": vocab}, device_id_type=MESH,
        )
        copy.start()
        sends.append((src, ss))

    def local(src, dst, sem):
        pltpu.make_async_copy(src, dst, sem).start()

    def arrived(dst, sem):
        pltpu.make_async_copy(dst, dst, sem).wait()

    def turn(s, base, size):
        return lax.rem(base + s, size)

    def columns(q, core):
        if F % 128 == 0:
            return w[:, pl.ds(pl.multiple_of((q * cpc + core) * F, F), F)]
        out = w[:, q * cpc * F:(q * cpc + 1) * F]
        for a in range(1, cpc):
            out = jnp.where(core == a, w[:, (q * cpc + a) * F:(q * cpc + a + 1) * F], out)
        return out

    row_order = list(range(1, n)) + [0]

    weight_in = pltpu.make_async_copy(w_in, w, io.at[0])
    weight_in.start()

    barrier = pltpu.get_barrier_semaphore()
    for s in range(1, nv):
        pl.semaphore_signal(barrier, inc=1, device_id={"dp": k, "vocab": turn(s, j, nv)}, device_id_type=MESH)
    for s in range(1, n):
        pl.semaphore_signal(barrier, inc=1, device_id={"dp": turn(s, k, n), "vocab": j}, device_id_type=MESH)
    pl.semaphore_wait(barrier, nv + n - 2)

    for h in range(nc):
        piece = hid.at[pl.ds(h * Tc, Tc)]
        for s in range(1, nz):
            to = turn(s, z, nz)
            push(piece, gat.at[z, h], h1_s.at[s, h], h1_r.at[z, h], k, to * cpc + c)
        local(piece, gat.at[z, h], h1_r.at[z, h])

    def exchange(h):
        for s in row_order:
            i = turn(s, k, n)
            for q in range(zpd):
                src = gat.at[i * zpd + q, h]
                arrived(src, h1_r.at[i * zpd + q, h])
                bl = q * cpc + c
                if s:
                    push(src, hb.at[bl, h, k], h2_s.at[s, q, h], hb_r.at[k, bl, h], i, j)
                else:
                    local(src, hb.at[bl, h, k], hb_r.at[k, bl, h])

    def partial(h):
        for s in [0] + list(range(1, n)):
            t = turn(s, k, n)
            for q in range(zpd):
                bl = q * cpc + c
                slot = hb.at[bl, h, t]
                arrived(slot, hb_r.at[t, bl, h])
                for d in range(1, cpc):
                    push(slot, slot, h3_s.at[s, q, d, h], hb_r.at[t, bl, h], k, z * cpc + turn(d, c, cpc))
        for s in [0] + list(range(1, n)):
            t = turn(s, k, n)
            for q in range(zpd):
                for d in range(1, cpc):
                    bl = q * cpc + turn(d, c, cpc)
                    arrived(hb.at[bl, h, t], hb_r.at[t, bl, h])
        total = dot_nt(hb[0, h].reshape(n * Tc, F), w[:, 0:F])
        for bl in range(1, bpd):
            total += dot_nt(hb[bl, h].reshape(n * Tc, F), w[:, bl * F:(bl + 1) * F])
        lp[h] = total.reshape(n, Tc, V)
        for s in range(1, n):
            t = turn(s, k, n)
            push(lp.at[h, t], lr.at[h, s - 1], l_s.at[s - 1, h], l_r.at[s - 1, h], t, j)

    exchange(0)
    weight_in.wait()
    for h in range(nc):
        if h + 1 < nc:
            exchange(h + 1)
        partial(h)
    rows = []
    for h in range(nc):
        own = lp[h, k]
        for s in range(n - 1):
            arrived(lr.at[h, s], l_r.at[s, h])
            own += lr[h, s]
        rows.append(own)
    logits = jnp.concatenate(rows, axis=0)

    def to_column(row):
        return jnp.transpose(jnp.broadcast_to(row, (128, T)))[:, :1]

    target_col = to_column(tgt[...].astype(f32)).astype(jnp.int32) - j * V
    onehot = lax.broadcasted_iota(jnp.int32, (T, V), 1) == target_col
    top = jnp.max(logits, axis=1, keepdims=True)
    part = jnp.sum(jnp.exp(logits - top), axis=1, keepdims=True)
    hit = jnp.sum(jnp.where(onehot, logits, 0.0), axis=1, keepdims=True)
    lane = lax.broadcasted_iota(jnp.int32, (T, 128), 1)
    packed = jnp.where(lane == 0, top, jnp.where(lane == 1, part, hit))
    mine = jnp.transpose(packed)[:8, :]
    st[...] = mine
    sr[j] = mine
    for s in range(1, nv):
        push(st, sr.at[j], s_s.at[s], s_r.at[j], k, turn(s, j, nv))
    for s in range(1, nv):
        frm = turn(s, j, nv)
        arrived(sr.at[frm], s_r.at[frm])
    stats = sr[...]
    tops, parts, hits = stats[:, 0, :], stats[:, 1, :], stats[:, 2, :]
    row_top = jnp.max(tops, axis=0, keepdims=True)
    exp_sum = jnp.sum(parts * jnp.exp(tops - row_top), axis=0, keepdims=True)
    target_logit = jnp.sum(hits, axis=0, keepdims=True)
    log_total = row_top + jnp.log(exp_sum)
    row_keep = keep[...].astype(f32)
    loss_out[...] = row_keep * (log_total - target_logit)

    soft = jnp.exp(logits - to_column(log_total))
    dl = (loss_scale * to_column(row_keep) * (soft - jnp.where(onehot, 1.0, 0.0))).astype(bf16)
    dall[:, k] = dl.reshape(nc, Tc, V)
    for s in range(1, n):
        push(dall.at[:, k], dall.at[:, k], d_s.at[s], d_r.at[k], turn(s, k, n), j)

    def other_part(s):
        t = turn(s, k, n)
        if s:
            arrived(dall.at[:, t], d_r.at[t])
        rows = dall[:, t].reshape(T, V)
        for d in range(1, cpc):
            other = turn(d, c, cpc)
            for q in range(zpd):
                ps[s, d - 1, q] = dot_nn(rows, columns(q, other))
            push(ps.at[s, d - 1], pr.at[s, d - 1], p_s.at[s, d - 1], p_r.at[s, d - 1], k, z * cpc + other)

    def relay(s, src, q, g):
        to = turn(s, k, n) * zpd + q
        dst = g2.at[z, pl.ds(g * Tg, Tg)]

        @pl.when(to != z)
        def _():
            pltpu.make_async_remote_copy(
                src_ref=src, dst_ref=dst, send_sem=g2_s.at[s, q, g], recv_sem=g2_r.at[z, g],
                device_id={"dp": k, "vocab": to * cpc + c}, device_id_type=MESH,
            ).start()

        @pl.when(to == z)
        def _():
            pltpu.make_async_copy(src, dst, g2_r.at[z, g]).start()

    def own_part(s):
        t = turn(s, k, n)
        rows = dall[:, t].reshape(T, V)
        for d in range(1, cpc):
            arrived(pr.at[s, d - 1], p_r.at[s, d - 1])
        for q in range(zpd):
            part_sum = dot_nn(rows, columns(q, c))
            for d in range(1, cpc):
                part_sum += pr[s, d - 1, q]
            gs[s, q] = part_sum.astype(bf16)
        for g in range(ng):
            if s:
                piece = gs.at[s, :, pl.ds(g * Tg, Tg)]
                push(piece, g1.at[k, :, pl.ds(g * Tg, Tg)], g1_s.at[s, g], g1_r.at[k, g], t, j)
            else:
                for q in range(zpd):
                    relay(0, gs.at[0, q, pl.ds(g * Tg, Tg)], q, g)

    other_part(0)
    own_part(0)
    for s in range(1, n):
        other_part(s)
        if s > 1:
            own_part(s - 1)
    own_part(n - 1)

    grads = jnp.transpose(dall[...].reshape(n * T, V))
    squares = jnp.zeros((1, F), f32)
    per = -(-bpd // n)
    done = 0
    for s in range(1, n + 1):
        for bl in range(done, min(done + per, bpd)):
            grad = dot_nn(grads, hb[bl].reshape(n * T, F))
            wg[:, bl * F:(bl + 1) * F] = grad.astype(bf16)
            squares += jnp.sum(grad * grad, axis=0, keepdims=True)
        done += per
        if s < n:
            i = turn(s, k, n)
            for g in range(ng):
                arrived(g1.at[i, :, pl.ds(g * Tg, Tg)], g1_r.at[i, g])
                for q in range(zpd):
                    relay(s, g1.at[i, q, pl.ds(g * Tg, Tg)], q, g)
    weight_out = pltpu.make_async_copy(wg, wg_out, io.at[1])
    weight_out.start()

    total = None
    for src in range(nz):
        for g in range(ng):
            arrived(g2.at[src, pl.ds(g * Tg, Tg)], g2_r.at[src, g])
        term = g2[src].astype(f32)
        total = term if total is None else total + term
    hg_out[...] = total.astype(bf16)

    both = jnp.sum(squares) + jnp.sum(total * total)
    value = jnp.full((8, 128), both, f32)
    n1s[...] = value
    n1[j] = value
    for s in range(1, nv):
        push(n1s, n1.at[j], n1_s.at[s], n1_r.at[j], k, turn(s, j, nv))
    for s in range(1, nv):
        frm = turn(s, j, nv)
        arrived(n1.at[frm], n1_r.at[frm])
    value = n1[0]
    for a in range(1, nv):
        value = value + n1[a]
    n2s[...] = value
    n2[k] = value
    for s in range(1, n):
        push(n2s, n2.at[k], n2_s.at[s], n2_r.at[k], turn(s, k, n), j)
    for s in range(1, n):
        frm = turn(s, k, n)
        arrived(n2.at[frm], n2_r.at[frm])
    value = n2[0]
    for a in range(1, n):
        value = value + n2[a]
    norm_out[...] = jnp.sqrt(value)

    for src, ss in sends:
        pltpu.make_async_copy(src, src, ss).wait()
    for s in range(n):
        i = turn(s, k, n)
        for q in range(zpd):
            @pl.when(i * zpd + q != z)
            def _():
                for g in range(ng):
                    piece = g2.at[0, pl.ds(0, Tg)]
                    pltpu.make_async_copy(piece, piece, g2_s.at[s, q, g]).wait()
    weight_out.wait()


def on_device(n, nv, hidden, weight, targets, loss_mask):
    T, F = hidden.shape
    R, V = weight.shape
    bpd = nv // n
    cpc = 2 if bpd % 2 == 0 else 1
    zpd, nz = bpd // cpc, nv // cpc
    nc = 4 if T % 64 == 0 else 1
    ng = 2 if T % 32 == 0 else 1
    dma = pltpu.SemaphoreType.DMA
    vmem = pl.BlockSpec(memory_space=pltpu.VMEM)
    hbm = pl.BlockSpec(memory_space=pl.ANY)
    others = max(cpc - 1, 1)
    hg, wg, loss, norm = pl.pallas_call(
        functools.partial(kernel, n, nv, cpc, nc, ng),
        out_shape=(
            jax.ShapeDtypeStruct((T, F), bf16),
            jax.ShapeDtypeStruct((V, R), bf16),
            jax.ShapeDtypeStruct((1, T), f32),
            jax.ShapeDtypeStruct((8, 128), f32),
        ),
        in_specs=[vmem, hbm, vmem, vmem],
        out_specs=(vmem, hbm, vmem, vmem),
        scratch_shapes=[
            pltpu.VMEM((V, R), bf16),
            pltpu.VMEM((V, R), bf16),
            pltpu.VMEM((nz, nc, T // nc, F), bf16),
            pltpu.VMEM((bpd, nc, n, T // nc, F), bf16),
            pltpu.VMEM((nc, n, T // nc, V), f32),
            pltpu.VMEM((nc, n - 1, T // nc, V), f32),
            pltpu.VMEM((8, T), f32),
            pltpu.VMEM((nv, 8, T), f32),
            pltpu.VMEM((nc, n, T // nc, V), bf16),
            pltpu.VMEM((n, others, zpd, T, F), f32),
            pltpu.VMEM((n, others, zpd, T, F), f32),
            pltpu.VMEM((n, zpd, T, F), bf16),
            pltpu.VMEM((n, zpd, T, F), bf16),
            pltpu.VMEM((nz, T, F), bf16),
            pltpu.VMEM((8, 128), f32),
            pltpu.VMEM((nv, 8, 128), f32),
            pltpu.VMEM((8, 128), f32),
            pltpu.VMEM((n, 8, 128), f32),
            dma((nz, nc)), dma((nz, nc)),
            dma((n, zpd, nc)), dma((n, bpd, nc)), dma((n, zpd, cpc, nc)),
            dma((n, nc)), dma((n, nc)),
            dma((nv,)), dma((nv,)),
            dma((n,)), dma((n,)),
            dma((2,)),
            dma((n, others)), dma((n, others)),
            dma((n, ng)), dma((n, ng)),
            dma((n, zpd, ng)), dma((nz, ng)),
            dma((nv,)), dma((nv,)),
            dma((n,)), dma((n,)),
        ],
        compiler_params=pltpu.CompilerParams(
            collective_id=0, has_side_effects=True, vmem_limit_bytes=60 * 1024 * 1024
        ),
    )(hidden, weight.T, targets.reshape(1, T), loss_mask.reshape(1, T))
    return hg, wg.T, loss.reshape(T), norm[0, 0]


def solution(mesh):
    placed = (P("dp", "vocab"), P("dp", "vocab"), P("dp"), P("dp"))
    return jax.shard_map(
        functools.partial(on_device, mesh.shape["dp"], mesh.shape["vocab"]),
        mesh=mesh,
        in_specs=placed,
        out_specs=(P("dp", "vocab"), P("dp", "vocab"), P("dp"), P()),
        check_vma=False,
    )
```

time: 139 us -> 120 us (0.86)
  Pallas kernels: 127 us -> 113 us
  local copies, waits for them, and re-layouts: 11.1 us -> 6.81 us
    pallas_call x1, Pallas kernels: 127 us -> 113 us  [on_device(): pl.pallas_call(functools.partial(kernel, n, nv, cpc, nc, ng), out_shape=(...]
    unnamed x8 -> x5, local copies, waits for them, and re-layouts: 9.9 us -> 5.62 us
where the time goes in v2:
time: 120 us
  Pallas kernels  113 us (94%)
  local copies, waits for them, and re-layouts  6.81 us (6%)
    pallas_call x1, Pallas kernels, on_device(): pl.pallas_call(functools.partial(kernel, n, nv, cpc, nc, ng), out_shape=(...  113 us
    unnamed x5, local copies, waits for them, and re-layouts  5.62 us

profile of v2, /device:TPU:0, one launch (start us, length us, event | category | flops | bytes accessed | tf_op | source)
XLA Modules:
  0.0 120.0 jit_solution(1368021917163113588)
XLA Ops:
  0.6 112.6 %shard_map.75 = (bf16[128,1024]{1,0:T(8,128)(2,1)}, bf16[594,2048]{1,0:T(8,128)(2,1)}, f32[1,128]{1,0:T(1,128)}, f32[8,128]{1,0:T(8,128)}) custom-call(bf16[128,1024]{1,0:T(8,128)(2,1)} %hid.1, bf16[594,2048]{1,0:T(8,128)(2,1)} %bitcast.6, s32[1,128]{1,0:T(1,128)} %bitcast.8, s32[1,128]{1,0:T(1,128)} %bitcast.9), custom_call_target="tpu_custom_call" | custom-call | tf_op jit(solution)/shard_map/pallas_call | solution.py:302
  113.2 1.2 slice.3
  114.4 1.7 %copy.11 = bf16[128,1024]{1,0:T(8,128)(2,1)} copy(bf16[128,1024]{1,0:T(8,128)(2,1)} %get-tuple-element.16) | data formatting | bytes 524288
  116.0 0.0 copy-start
  116.1 3.4 %copy.12 = bf16[2048,594]{0,1:T(8,128)(2,1)} copy(bf16[2048,594]{0,1:T(8,128)(2,1)} %bitcast.7) | data formatting | bytes 4866048
  119.5 0.0 copy-done
  119.5 0.5 copy.13
Async XLA Ops:
  116.0 3.4 %copy-start = (f32[1,128]{1,0:T(1,128)S(1)}, f32[1,128]{1,0:T(1,128)}, u32[]{:S(2)}) copy-start(f32[1,128]{1,0:T(1,128)} %get-tuple-element.10) | copy-start | bytes 1540

commit v3 on v2

--- a/solution.py
+++ b/solution.py
@@ -168,11 +168,20 @@
     soft = jnp.exp(logits - to_column(log_total))
     dl = (loss_scale * to_column(row_keep) * (soft - jnp.where(onehot, 1.0, 0.0))).astype(bf16)
     dall[:, k] = dl.reshape(nc, Tc, V)
-    for s in range(1, n):
-        push(dall.at[:, k], dall.at[:, k], d_s.at[s], d_r.at[k], turn(s, k, n), j)
+
+    shift = [0] + [1 + lax.rem(z + m, n - 1) for m in range(n - 1)]
+
+    def ahead(s):
+        return turn(shift[s], k, n)
+
+    def behind(s):
+        return turn(n - shift[s], k, n)
+
+    for s in range(1, n):
+        push(dall.at[:, k], dall.at[:, k], d_s.at[s], d_r.at[k], behind(s), j)
 
     def other_part(s):
-        t = turn(s, k, n)
+        t = ahead(s)
         if s:
             arrived(dall.at[:, t], d_r.at[t])
         rows = dall[:, t].reshape(T, V)
@@ -183,7 +192,7 @@
             push(ps.at[s, d - 1], pr.at[s, d - 1], p_s.at[s, d - 1], p_r.at[s, d - 1], k, z * cpc + other)
 
     def relay(s, src, q, g):
-        to = turn(s, k, n) * zpd + q
+        to = behind(s) * zpd + q
         dst = g2.at[z, pl.ds(g * Tg, Tg)]
 
         @pl.when(to != z)
@@ -198,7 +207,7 @@
             pltpu.make_async_copy(src, dst, g2_r.at[z, g]).start()
 
     def own_part(s):
-        t = turn(s, k, n)
+        t = ahead(s)
         rows = dall[:, t].reshape(T, V)
         for d in range(1, cpc):
             arrived(pr.at[s, d - 1], p_r.at[s, d - 1])
@@ -234,7 +243,7 @@
             squares += jnp.sum(grad * grad, axis=0, keepdims=True)
         done += per
         if s < n:
-            i = turn(s, k, n)
+            i = behind(s)
             for g in range(ng):
                 arrived(g1.at[i, :, pl.ds(g * Tg, Tg)], g1_r.at[i, g])
                 for q in range(zpd):
@@ -277,7 +286,7 @@
     for src, ss in sends:
         pltpu.make_async_copy(src, src, ss).wait()
     for s in range(n):
-        i = turn(s, k, n)
+        i = behind(s)
         for q in range(zpd):
             @pl.when(i * zpd + q != z)
             def _():

time: 120 us -> 114 us (0.950)
  Pallas kernels: 113 us -> 106 us
    pallas_call x1, Pallas kernels: 113 us -> 106 us  [on_device(): pl.pallas_call(functools.partial(kernel, n, nv, cpc, nc, ng), out_shape=(...]
where the time goes in v3:
time: 114 us
  Pallas kernels  106 us (93%)
  local copies, waits for them, and re-layouts  6.81 us (6%)
    pallas_call x1, Pallas kernels, on_device(): pl.pallas_call(functools.partial(kernel, n, nv, cpc, nc, ng), out_shape=(...  106 us
    unnamed x5, local copies, waits for them, and re-layouts  5.62 us

profile of v3, /device:TPU:0, one launch (start us, length us, event | category | flops | bytes accessed | tf_op | source)
XLA Modules:
  0.0 113.9 jit_solution(15743347044598756576)
XLA Ops:
  0.6 106.5 %shard_map.75 = (bf16[128,1024]{1,0:T(8,128)(2,1)}, bf16[594,2048]{1,0:T(8,128)(2,1)}, f32[1,128]{1,0:T(1,128)}, f32[8,128]{1,0:T(8,128)}) custom-call(bf16[128,1024]{1,0:T(8,128)(2,1)} %hid.1, bf16[594,2048]{1,0:T(8,128)(2,1)} %bitcast.6, s32[1,128]{1,0:T(1,128)} %bitcast.8, s32[1,128]{1,0:T(1,128)} %bitcast.9), custom_call_target="tpu_custom_call" | custom-call | tf_op jit(solution)/shard_map/pallas_call | solution.py:311
  107.1 1.2 %slice.3 = f32[1,1]{1,0:T(1,128)} slice(f32[8,128]{1,0:T(8,128)} %get-tuple-element.11), slice={[0:1], [0:1]} | slice | bytes 8 | tf_op jit(solution)/shard_map/slice | solution.py:356
  108.3 1.7 %copy.11 = bf16[128,1024]{1,0:T(8,128)(2,1)} copy(bf16[128,1024]{1,0:T(8,128)(2,1)} %get-tuple-element.16) | data formatting | bytes 524288
  109.9 0.0 copy-start
  110.0 3.4 %copy.12 = bf16[2048,594]{0,1:T(8,128)(2,1)} copy(bf16[2048,594]{0,1:T(8,128)(2,1)} %bitcast.7) | data formatting | bytes 4866048
  113.4 0.0 copy-done
  113.4 0.5 copy.13
Async XLA Ops:
  109.9 3.4 %copy-start = (f32[1,128]{1,0:T(1,128)S(1)}, f32[1,128]{1,0:T(1,128)}, u32[]{:S(2)}) copy-start(f32[1,128]{1,0:T(1,128)} %get-tuple-element.10) | copy-start | bytes 1540
